TPU v7x, 32 devices: a whole 2x2x4 slice. The times are simulated.
32 devices in a mesh: batch: 4 (over x, core), seq: 8 (over z, y).
Axes of the slice: x: 2, y: 2, z: 4, core: 2. Of those that a mesh axis runs over, the one named last changes fastest.
Arguments:
- tokens: bfloat16 [16, 2048, 768], P('batch', 'seq'), may hold values from -6 to 6
- prompts: float32 [50, 768], replicated, may hold values from -6 to 6
- image_id: int32 [16, 2048], P('batch'), may hold values from 0 to 8, as said below
- prompt_slot: int32 [16, 2048], P('batch', 'seq'), may hold values from 0 to 50, as said below
- ln1_gain: float32 [768], replicated, may hold values from 0.5 to 1.5
- ln1_bias: float32 [768], replicated, may hold values from -1.8 to 1.8
- w_qkv: bfloat16 [768, 2304], replicated, may hold values from -0.21875 to 0.21875
- bias_qv: float32 [1536], replicated, may hold values from -1.8 to 1.8
- w_out: bfloat16 [768, 768], replicated, may hold values from -0.875 to 0.875
- bias_out: float32 [768], replicated, may hold values from -1.8 to 1.8
- ln2_gain: float32 [768], replicated, may hold values from 0.5 to 1.5
- ln2_bias: float32 [768], replicated, may hold values from -1.8 to 1.8
- w_up: bfloat16 [768, 3072], replicated, may hold values from -0.21875 to 0.21875
- bias_up: float32 [3072], replicated, may hold values from -1.8 to 1.8
- w_down: bfloat16 [3072, 768], replicated, may hold values from -0.109375 to 0.109375
- bias_down: float32 [768], replicated, may hold values from -1.8 to 1.8
- cotangent: bfloat16 [16, 2048, 768], P('batch', 'seq'), may hold values from -6 to 6
Outputs:
- output: bfloat16 [16, 2048, 768], P('batch', 'seq')
- token_gradient: bfloat16 [16, 2048, 768], P('batch', 'seq')
- prompt_gradient: float32 [50, 768], replicated
Inputs may be any that keep to these rules, and one draw needn't show every extreme that they name: `image_id`: each row holds 8 runs of 247 consecutive positions with ids 0 to 7 in order; all other positions (padding, some before, between or after the runs) have id 8. `prompt_slot`: within each run of image_id, the first position is the class token, the next 50 carry slots 0 to 49 in order; class tokens, patches and padding carry 50.
All inputs are finite; a program needn't handle non-finite values.
Results may differ from a plain program's by a relative error of at most 0.012.
Values may be sent and summed in bfloat16 or wider, within the bound.
A program may use at most 384 MiB of HBM per device.

v0:
```python
import jax
import jax.numpy as jnp
from jax import lax
from jax.sharding import PartitionSpec as P

ATTENTION_HEADS = 12
HEAD_FEATURES = 64
PROMPTS = 50
IMAGES_PER_ROW = 8
IMAGE_TOKENS = 247


def passed_along(block, axis, distance):
    devices = range(lax.axis_size(axis))
    route = [(i - distance, i) for i in devices if i - distance in devices]
    return lax.ppermute(block, axis, route)


def normalize(value_rows):
    mean = jnp.mean(value_rows, axis=-1, keepdims=True)
    centered = value_rows - mean
    inverse = lax.rsqrt(jnp.mean(centered * centered, axis=-1, keepdims=True) + 1e-06)
    return (centered * inverse, inverse)


def norm_back(grad_in, normal_draws, inverse, gain):
    scaled = grad_in * gain
    return inverse * (
        scaled
        - jnp.mean(scaled, axis=-1, keepdims=True)
        - normal_draws * jnp.mean(scaled * normal_draws, axis=-1, keepdims=True)
    )


def block_rows(rows, span):
    group = min(rows, max(1, 512 // span))
    while rows % group:
        group = group - 1
    return group


def masked_scores(query_rows, key_rows, query_ids, key_ids, own_pos, key_pos):
    scores = jnp.einsum(
        "gqhd,gkhd->ghqk", query_rows, key_rows, preferred_element_type=jnp.float32
    ) * HEAD_FEATURES ** (-0.5)
    same_image = (query_ids[:, :, None] == key_ids[:, None, :]) & (query_ids < IMAGES_PER_ROW)[
        :, :, None
    ]
    permitted_mask = same_image | (own_pos[:, None] == key_pos[None, :])[None]
    return jnp.where(permitted_mask[:, None], scores, -1e30)


def body(
    tokens,
    prompts,
    image_id,
    prompt_slot,
    ln1_gain,
    ln1_bias,
    w_qkv,
    bias_qv,
    w_out,
    bias_out,
    ln2_gain,
    ln2_bias,
    w_up,
    bias_up,
    w_down,
    bias_down,
    cotangent,
):
    rows, span, width = tokens.shape
    length = image_id.shape[1]
    start = lax.axis_index("seq") * span
    own_ids = lax.dynamic_slice_in_dim(image_id, start, span, 1)
    own_pos = start + jnp.arange(span, dtype=jnp.int32)
    valid = (own_ids < IMAGES_PER_ROW).astype(jnp.float32)
    one_hot = (prompt_slot[..., None] == jnp.arange(PROMPTS, dtype=jnp.int32)).astype(jnp.float32)
    placed = jnp.einsum("rsn,nd->rsd", one_hot, prompts, precision=lax.Precision.HIGHEST)
    is_prompt = (prompt_slot < PROMPTS)[..., None]
    inserted = jnp.where(is_prompt, placed, tokens.astype(jnp.float32))
    normal1, inverse1 = normalize(inserted)
    normed1 = (normal1 * ln1_gain + ln1_bias).astype(jnp.bfloat16)
    bias_three = jnp.concatenate(
        [bias_qv[:width], jnp.zeros((width,), jnp.float32), bias_qv[width:]]
    )
    query_key_value = (
        jnp.einsum("rsd,de->rse", normed1, w_qkv, preferred_element_type=jnp.float32) + bias_three
    ).astype(jnp.bfloat16)
    query_rows = query_key_value[..., :width]
    key_own = query_key_value[..., width : 2 * width]
    value_own = query_key_value[..., 2 * width :]
    reach = (IMAGE_TOKENS - 2 + span) // span
    offsets = list(range(-reach, reach + 1))
    key_parts = []
    value_parts = []
    for offset in offsets:
        if offset == 0:
            fetched_key, fetched_value = (key_own, value_own)
        else:
            fetched_key, fetched_value = passed_along((key_own, value_own), "seq", -offset)
        key_parts.append(fetched_key)
        value_parts.append(fetched_value)
    key_rows = jnp.concatenate(key_parts, axis=1)
    value_rows = jnp.concatenate(value_parts, axis=1)
    raw_pos = jnp.concatenate(
        [start + offset * span + jnp.arange(span, dtype=jnp.int32) for offset in offsets]
    )
    in_row = (raw_pos >= 0) & (raw_pos < length)
    taken = jnp.take(image_id, jnp.clip(raw_pos, 0, length - 1), axis=1)
    key_ids = jnp.where(in_row[None, :], taken, -1)
    key_pos = jnp.where(in_row, raw_pos, -1)
    key_count = key_rows.shape[1]
    group = block_rows(rows, span)

    def grouped(array):
        return array.reshape((rows // group, group) + array.shape[1:])

    query_heads = grouped(query_rows.reshape(rows, span, ATTENTION_HEADS, HEAD_FEATURES))
    key_heads = grouped(key_rows.reshape(rows, key_count, ATTENTION_HEADS, HEAD_FEATURES))
    value_heads = grouped(value_rows.reshape(rows, key_count, ATTENTION_HEADS, HEAD_FEATURES))
    query_ids = grouped(own_ids)
    grouped_key_ids = grouped(key_ids)

    def forward_block(inputs):
        query_blk, key_blk, value_blk, qid_blk, kid_blk = inputs
        scores = masked_scores(query_blk, key_blk, qid_blk, kid_blk, own_pos, key_pos)
        row_top = jnp.max(scores, axis=-1, keepdims=True)
        total = jnp.sum(jnp.exp(scores - row_top), axis=-1, keepdims=True)
        log_total = row_top + jnp.log(total)
        attention_weights = jnp.exp(scores - log_total).astype(jnp.bfloat16)
        attention_output = jnp.einsum(
            "vbta,vabj->vtbj", attention_weights, value_blk, preferred_element_type=jnp.float32
        )
        return (attention_output.astype(jnp.bfloat16), log_total[..., 0])

    attention_output, log_totals = lax.map(
        forward_block, (query_heads, key_heads, value_heads, query_ids, grouped_key_ids)
    )
    attention_output = attention_output.reshape(rows, span, width)
    hidden1 = (
        inserted
        + jnp.einsum("rsd,de->rse", attention_output, w_out, preferred_element_type=jnp.float32)
        + bias_out
    )
    normal2, inverse2 = normalize(hidden1)
    normed2 = (normal2 * ln2_gain + ln2_bias).astype(jnp.bfloat16)
    upper = jnp.einsum("rsd,df->rsf", normed2, w_up, preferred_element_type=jnp.float32) + bias_up
    activated, gelu_pull = jax.vjp(lambda inner: jax.nn.gelu(inner, approximate=False), upper)
    activated = activated.astype(jnp.bfloat16)
    output = (
        hidden1
        + jnp.einsum("rsf,fd->rsd", activated, w_down, preferred_element_type=jnp.float32)
        + bias_down
    ).astype(jnp.bfloat16)
    out_grad = cotangent.astype(jnp.float32) * valid[..., None]
    act_grad = jnp.einsum(
        "rsd,fd->rsf", out_grad.astype(jnp.bfloat16), w_down, preferred_element_type=jnp.float32
    )
    upper_grad = gelu_pull(act_grad)[0].astype(jnp.bfloat16)
    normed2_grad = jnp.einsum("rsf,df->rsd", upper_grad, w_up, preferred_element_type=jnp.float32)
    hidden1_grad = out_grad + norm_back(normed2_grad, normal2, inverse2, ln2_gain)
    attended_grad = jnp.einsum(
        "rse,de->rsd", hidden1_grad.astype(jnp.bfloat16), w_out, preferred_element_type=jnp.float32
    ).astype(jnp.bfloat16)
    attended_grad = grouped(attended_grad.reshape(rows, span, ATTENTION_HEADS, HEAD_FEATURES))

    def backward_block(inputs):
        query_blk, key_blk, value_blk, qid_blk, kid_blk, total_blk, grad_blk = inputs
        scores = masked_scores(query_blk, key_blk, qid_blk, kid_blk, own_pos, key_pos)
        attention_weights = jnp.exp(scores - total_blk[..., None])
        value_grad = jnp.einsum(
            "ghqk,gqhd->gkhd",
            attention_weights.astype(jnp.bfloat16),
            grad_blk,
            preferred_element_type=jnp.float32,
        )
        prob_grad = jnp.einsum(
            "gqhd,gkhd->ghqk", grad_blk, value_blk, preferred_element_type=jnp.float32
        )
        inner = jnp.sum(attention_weights * prob_grad, axis=-1, keepdims=True)
        score_grad = (attention_weights * (prob_grad - inner)).astype(jnp.bfloat16)
        query_grad = jnp.einsum(
            "vbta,vabj->vtbj", score_grad, key_blk, preferred_element_type=jnp.float32
        ) * HEAD_FEATURES ** (-0.5)
        key_grad = jnp.einsum(
            "ghqk,gqhd->gkhd", score_grad, query_blk, preferred_element_type=jnp.float32
        ) * HEAD_FEATURES ** (-0.5)
        return (query_grad, key_grad, value_grad)

    query_grad, key_grad, value_grad = lax.map(
        backward_block,
        (
            query_heads,
            key_heads,
            value_heads,
            query_ids,
            grouped_key_ids,
            log_totals,
            attended_grad,
        ),
    )
    query_grad = query_grad.reshape(rows, span, width)
    key_grad = key_grad.reshape(rows, key_count, width)
    value_grad = value_grad.reshape(rows, key_count, width)
    key_total = key_grad[:, reach * span : (reach + 1) * span]
    value_total = value_grad[:, reach * span : (reach + 1) * span]
    for offset in range(-reach, reach + 1):
        if offset != 0:
            first = (offset + reach) * span
            back_key, back_value = (
                passed_along(
                    key_grad[:, first : first + span].astype(jnp.bfloat16), "seq", offset
                ).astype(jnp.float32),
                passed_along(
                    value_grad[:, first : first + span].astype(jnp.bfloat16), "seq", offset
                ).astype(jnp.float32),
            )
            key_total = key_total + back_key
            value_total = value_total + back_value
    qkv_grad = jnp.concatenate([query_grad, key_total, value_total], axis=-1).astype(jnp.bfloat16)
    normed1_grad = jnp.einsum("rse,de->rsd", qkv_grad, w_qkv, preferred_element_type=jnp.float32)
    inserted_grad = hidden1_grad + norm_back(normed1_grad, normal1, inverse1, ln1_gain)
    token_gradient = jnp.where(is_prompt, 0.0, inserted_grad).astype(jnp.bfloat16)
    prompt_part = jnp.einsum("rsn,rsd->nd", one_hot, inserted_grad, precision=lax.Precision.HIGHEST)
    prompt_gradient = lax.psum(prompt_part, ("batch", "seq"))
    return (output, token_gradient, prompt_gradient)


def solution(mesh):
    in_specs = (
        P("batch", "seq", None),
        P(),
        P("batch", None),
        P("batch", "seq"),
        P(),
        P(),
        P(),
        P(),
        P(),
        P(),
        P(),
        P(),
        P(),
        P(),
        P(),
        P(),
        P("batch", "seq", None),
    )
    out_specs = (P("batch", "seq", None), P("batch", "seq", None), P())
    return jax.shard_map(body, mesh=mesh, in_specs=in_specs, out_specs=out_specs, check_vma=False)
```

profile of v0, /device:TPU:8, one launch (start us, length us, event | category | flops | bytes accessed | tf_op | source)
XLA Modules:
  0.0 715.2 jit_solution(10487192284243288981)
XLA Ops:
  45.8 81.3 %collective-permute-done.3 = bf16[4,256,768]{2,1,0:T(8,128)(2,1)} collective-permute-done((bf16[4,256,768]{2,1,0:T(8,128)(2,1)}, bf16[4,256,768]{2,1,0:T(8,128)(2,1)}, u32[]{:S(2)}, u32[]{:S(2)}) %collective-permute-start.3) | collective-permute-done | bytes 1572896 | tf_op jit(solution)/shard_map/ppermute | solution.py:16
  131.0 6.6 copy.37
  137.6 22.0 %collective-permute-done.1 = bf16[4,256,768]{2,1,0:T(8,128)(2,1)} collective-permute-done((bf16[4,256,768]{2,1,0:T(8,128)(2,1)}, bf16[4,256,768]{2,1,0:T(8,128)(2,1)}, u32[]{:S(2)}, u32[]{:S(2)}) %collective-permute-start.1) | collective-permute-done | bytes 1572896 | tf_op jit(solution)/shard_map/ppermute | solution.py:16
  163.6 6.6 copy.33
  170.2 47.5 %while.28 = (s32[]{:T(128)}, bf16[2,2,256,12,64]{2,4,3,1,0:T(8,128)(2,1)}, f32[2,2,12,256]{3,2,1,0:T(8,128)}, bf16[2,2,768,12,64]{2,4,3,1,0:T(8,128)(2,1)}, s32[...) while((s32[]{:T(128)}, ...), condition=%wide.region_5.6_spmd.clone, body=%wide.region_2.5_spmd.clone.sunk | while | flops 1261628160 | bytes 141033712 | solution.py:137
  183.3 10.4 %fusion.152 = bf16[2,2,256,12,64]{2,4,3,1,0:T(8,128)(2,1)} fusion(bf16[2,2,256,12,64]{2,4,3,1,0:T(8,128)(2,1)} %get-tuple-element.464, s32[]{:T(128)S(6)} %copy.54, f32[2,12,256,768]{3,2,1,0:T(8,128)} %copy-done.2, f32[2,12,256]{2,1,0:T(8,128)S(1)} %get-tuple-element.433, pred[2,256,768]{2,1,0:T(8,128)(4,1)S(1)} %and_or_fusion.4, ...), kind=kOutput, calls=%fused_computation.17.clone.1 | convolution fusion | flops 623247360 | bytes 22438912 | tf_op jit(solution)/shard_map/while/body/eval_jaxpr/vbta,vabj->vtbj/dot_general | solution.py:132
  206.9 10.4 %fusion.152 = bf16[2,2,256,12,64]{2,4,3,1,0:T(8,128)(2,1)} fusion(bf16[2,2,256,12,64]{2,4,3,1,0:T(8,128)(2,1)} %get-tuple-element.464, s32[]{:T(128)S(6)} %copy.54, f32[2,12,256,768]{3,2,1,0:T(8,128)} %copy-done.2, f32[2,12,256]{2,1,0:T(8,128)S(1)} %get-tuple-element.433, pred[2,256,768]{2,1,0:T(8,128)(4,1)S(1)} %and_or_fusion.4, ...), kind=kOutput, calls=%fused_computation.17.clone.1 | convolution fusion | flops 623247360 | bytes 22438912 | tf_op jit(solution)/shard_map/while/body/eval_jaxpr/vbta,vabj->vtbj/dot_general | solution.py:132
  222.8 11.3 %fusion.95 = (u8[256,3072]{1,0:T(8,128)(4,1)S(1)}, u8[256,3072]{1,0:T(8,128)(4,1)S(1)}, f32[4,256,3072]{2,1,0:T(8,128)S(1)}) fusion(f32[3072]{0:T(1024)S(1)} %copy-done.29, bf16[768,3072]{1,0:T(8,128)(2,1)} %param.33, f32[4,256,768]{2,1,0:T(8,128)S(1)} %get-tuple-element.285, f32[768]{0:T(1024)S(1)} %copy-done.39, f32[768]{0:T(1024)S(1)} %copy-done.36, ...), kind=kOutput, calls=%fused_computation.138 | convolution fusion | flops 4878237696 | bytes 22046720 | tf_op jit(solution)/shard_map/rsd,df->rsf/dot_general | solution.py:148
  234.1 28.7 %fusion.63 = f32[4,256,3072]{2,1,0:T(8,128)} fusion(f32[4,256,3072]{2,1,0:T(8,128)S(1)} %get-tuple-element.286, f32[3072]{0:T(1024)S(1)} %copy-done.29, u8[256,3072]{1,0:T(8,128)(4,1)S(1)} %get-tuple-element.206, u8[256,3072]{1,0:T(8,128)(4,1)S(1)} %get-tuple-element.205), kind=kLoop, calls=%fused_computation.76 | loop fusion | flops 213909504 | bytes 26750976 | tf_op jit(solution)/shard_map/jvp()/erfc | solution.py:149
  262.8 20.7 %multiply_reduce_fusion.6 = (f32[4,256]{1,0:T(4,128)}, f32[4,256]{1,0:T(4,128)}, f32[4,256,768]{2,1,0:T(8,128)}) fusion(f32[768]{0:T(1024)} %param.31, f32[4,256]{1,0:T(4,128)} %copy-done.21, f32[4,256,768]{2,1,0:T(8,128)} %copy-done.6, f32[4,256]{1,0:T(4,128)} %copy-done.16, bf16[768,3072]{1,0:T(8,128)(2,1)} %param.33, f32[4,256,3072]{2,1,0:T(8,128)} %fusion.63, ...), kind=kOutput, calls=%fused_computation.142 | convolution fusion | flops 9717938176 | bytes 42503168 | tf_op jit(solution)/shard_map/rsf,df->rsd/dot_general | solution.py:161
  285.5 7.0 convolution_convert_fusion
  295.0 114.5 %while.29 = (s32[]{:T(128)}, bf16[2,2,256,12,64]{2,4,3,1,0:T(8,128)(2,1)}, f32[2,2,768,12,64]{2,4,3,1,0:T(8,128)}, f32[2,2,768,12,64]{2,4,3,1,0:T(8,128)}, bf16[...) while((s32[]{:T(128)}, ...), condition=%wide.region_12.13_spmd.clone, body=%wide.region_10.12_spmd.clone.sunk | while | flops 3093621504 | bytes 260910336 | solution.py:191
  308.2 7.7 %bitcast_dynamic-update-slice_fusion.11 = f32[2,2,768,12,64]{2,4,3,1,0:T(8,128)} fusion(f32[2,2,768,12,64]{2,4,3,1,0:T(8,128)} %get-tuple-element.502, s32[]{:T(128)S(6)} %copy.64, f32[2,12,256,768]{3,2,1,0:T(8,128)S(1)} %fusion.161, f32[2,12,256]{2,1,0:T(8,128)S(1)} %dynamic-slice_bitcast_fusion.9, pred[2,256,768]{2,1,0:T(8,128)(4,1)S(1)} %and_or_fusion.5, ...), kind=kOutput, calls=%fused_computation.40.clone.1 | convolution fusion | flops 622854144 | bytes 24798208 | tf_op jit(solution)/shard_map/while/body/eval_jaxpr/ghqk,gqhd->gkhd/dot_general | solution.py:172
  315.9 15.0 %multiply_reduce_fusion.8 = (f32[2,12,256]{2,1,0:T(8,128)S(1)}, f32[2,12,256,768]{3,2,1,0:T(8,128)}) fusion(f32[2,12,256,768]{3,2,1,0:T(8,128)} %copy-done.1, f32[2,12,256]{2,1,0:T(8,128)S(1)} %dynamic-slice_bitcast_fusion.9, pred[2,256,768]{2,1,0:T(8,128)(4,1)S(1)} %and_or_fusion.5, bf16[2,2,768,12,64]{2,4,3,1,0:T(8,128)(2,1)} %get-tuple-element.524, ...), kind=kOutput, calls=%fused_computation.32.clone.1 | convolution fusion | flops 627566592 | bytes 41337856 | tf_op jit(solution)/shard_map/while/body/eval_jaxpr/gqhd,gkhd->ghqk/dot_general | solution.py:178
  330.9 13.5 %multiply_convert_fusion.6 = bf16[2,12,256,768]{3,2,1,0:T(8,128)(2,1)S(1)} fusion(f32[2,12,256,768]{3,2,1,0:T(8,128)} %get-tuple-element.450, f32[2,12,256,768]{3,2,1,0:T(8,128)} %copy-done.1, f32[2,12,256]{2,1,0:T(8,128)S(1)} %get-tuple-element.451, f32[2,12,256]{2,1,0:T(8,128)S(1)} %dynamic-slice_bitcast_fusion.9, ...), kind=kLoop, calls=%fused_computation.31.clone.1 | loop fusion | flops 28311552 | bytes 47628288 | tf_op jit(solution)/shard_map/while/body/eval_jaxpr/convert_element_type | solution.py:182
  365.3 7.7 %bitcast_dynamic-update-slice_fusion.11 = f32[2,2,768,12,64]{2,4,3,1,0:T(8,128)} fusion(f32[2,2,768,12,64]{2,4,3,1,0:T(8,128)} %get-tuple-element.502, s32[]{:T(128)S(6)} %copy.64, f32[2,12,256,768]{3,2,1,0:T(8,128)S(1)} %fusion.161, f32[2,12,256]{2,1,0:T(8,128)S(1)} %dynamic-slice_bitcast_fusion.9, pred[2,256,768]{2,1,0:T(8,128)(4,1)S(1)} %and_or_fusion.5, ...), kind=kOutput, calls=%fused_computation.40.clone.1 | convolution fusion | flops 622854144 | bytes 24798208 | tf_op jit(solution)/shard_map/while/body/eval_jaxpr/ghqk,gqhd->gkhd/dot_general | solution.py:172
  372.9 15.0 %multiply_reduce_fusion.8 = (f32[2,12,256]{2,1,0:T(8,128)S(1)}, f32[2,12,256,768]{3,2,1,0:T(8,128)}) fusion(f32[2,12,256,768]{3,2,1,0:T(8,128)} %copy-done.1, f32[2,12,256]{2,1,0:T(8,128)S(1)} %dynamic-slice_bitcast_fusion.9, pred[2,256,768]{2,1,0:T(8,128)(4,1)S(1)} %and_or_fusion.5, bf16[2,2,768,12,64]{2,4,3,1,0:T(8,128)(2,1)} %get-tuple-element.524, ...), kind=kOutput, calls=%fused_computation.32.clone.1 | convolution fusion | flops 627566592 | bytes 41337856 | tf_op jit(solution)/shard_map/while/body/eval_jaxpr/gqhd,gkhd->ghqk/dot_general | solution.py:178
  388.0 13.5 %multiply_convert_fusion.6 = bf16[2,12,256,768]{3,2,1,0:T(8,128)(2,1)S(1)} fusion(f32[2,12,256,768]{3,2,1,0:T(8,128)} %get-tuple-element.450, f32[2,12,256,768]{3,2,1,0:T(8,128)} %copy-done.1, f32[2,12,256]{2,1,0:T(8,128)S(1)} %get-tuple-element.451, f32[2,12,256]{2,1,0:T(8,128)S(1)} %dynamic-slice_bitcast_fusion.9, ...), kind=kLoop, calls=%fused_computation.31.clone.1 | loop fusion | flops 28311552 | bytes 47628288 | tf_op jit(solution)/shard_map/while/body/eval_jaxpr/convert_element_type | solution.py:182
  409.5 9.6 %copy.42 = f32[4,768,768]{2,1,0:T(8,128)} copy(f32[4,768,768]{1,2,0:T(8,128)} %bitcast.177) | data formatting | bytes 18874368 | tf_op jit(solution)/shard_map/reshape | solution.py:205
  431.4 9.7 %copy.40 = f32[4,768,768]{2,1,0:T(8,128)} copy(f32[4,768,768]{1,2,0:T(8,128)} %bitcast.178) | data formatting | bytes 18874368 | tf_op jit(solution)/shard_map/reshape | solution.py:204
  456.4 76.0 %collective-permute-done.6 = bf16[4,256,768]{2,1,0:T(8,128)(2,1)} collective-permute-done((bf16[4,256,768]{2,1,0:T(8,128)(2,1)}, bf16[4,256,768]{2,1,0:T(8,128)(2,1)}, u32[]{:S(2)}, u32[]{:S(2)}) %collective-permute-start.6) | collective-permute-done | bytes 1572896 | tf_op jit(solution)/shard_map/ppermute | solution.py:16
  535.8 29.7 %collective-permute-done.4 = bf16[4,256,768]{2,1,0:T(8,128)(2,1)} collective-permute-done((bf16[4,256,768]{2,1,0:T(8,128)(2,1)}, bf16[4,256,768]{2,1,0:T(8,128)(2,1)}, u32[]{:S(2)}, u32[]{:S(2)}) %collective-permute-start.4) | collective-permute-done | bytes 1572896 | tf_op jit(solution)/shard_map/ppermute | solution.py:16
  578.7 14.3 %add_convert_fusion.3 = bf16[4,256,768]{2,1,0:T(8,128)(2,1)} fusion(f32[4,256,768]{2,1,0:T(8,128)} %copy-done.6, bf16[3072,768]{1,0:T(8,128)(2,1)} %param.35, f32[4,256,3072]{2,1,0:T(8,128)} %fusion.63, f32[4,256,3072]{2,1,0:T(8,128)} %copy-done.8, f32[3072]{0:T(1024)S(1)} %copy-done.30, f32[768]{0:T(1024)S(1)} %copy-done.40), kind=kOutput, calls=%fused_computation.130 | convolution fusion | flops 4846780416 | bytes 34618368 | tf_op jit(solution)/shard_map/rsf,fd->rsd/dot_general | solution.py:153
  593.0 113.5 %all-reduce.2.cloned.1.call-done = f32[50,768]{1,0:T(8,128)} async-done(((f32[50,768]{1,0:T(8,128)}), f32[50,768]{1,0:T(8,128)}) %all-reduce.2.cloned.1.call-update) | async-done | bytes 153616 | tf_op jit(solution)/shard_map/psum | solution.py:226
  (200 shorter events, 169.1 us)
Async XLA Ops:
  7.2 699.4 %all-reduce.2.cloned.1.call-start = ((), (), s32[]{:S(2)}) async-start(), calls=%async_computation | async-start | bytes 344064 | tf_op jit(solution)/shard_map/psum | solution.py:226
  20.2 106.9 %collective-permute-start.3 = (bf16[4,256,768]{2,1,0:T(8,128)(2,1)}, bf16[4,256,768]{2,1,0:T(8,128)(2,1)}, u32[]{:S(2)}, u32[]{:S(2)}) collective-permute-start(bf16[4,256,768]{2,1,0:T(8,128)(2,1)} %get-tuple-element.275), channel_id=1, source_target_pairs={{1,0},{2,1},{3,2},{4,3},{5,4},{6,5},{7,6},{9,8},{10,9},{11,10},{12... | collective-permute-start | bytes 4718600 | tf_op jit(solution)/shard_map/ppermute | solution.py:16
  23.5 103.6 %collective-permute-start.2 = (bf16[4,256,768]{2,1,0:T(8,128)(2,1)}, bf16[4,256,768]{2,1,0:T(8,128)(2,1)}, u32[]{:S(2)}, u32[]{:S(2)}) collective-permute-start(bf16[4,256,768]{2,1,0:T(8,128)(2,1)} %get-tuple-element.275), channel_id=1, source_target_pairs={{0,1},{1,2},{2,3},{3,4},{4,5},{5,6},{6,7},{8,9},{9,10},{10,11},{11... | collective-permute-start | bytes 4718600 | tf_op jit(solution)/shard_map/ppermute | solution.py:16
  26.0 133.6 %collective-permute-start.1 = (bf16[4,256,768]{2,1,0:T(8,128)(2,1)}, bf16[4,256,768]{2,1,0:T(8,128)(2,1)}, u32[]{:S(2)}, u32[]{:S(2)}) collective-permute-start(bf16[4,256,768]{2,1,0:T(8,128)(2,1)} %get-tuple-element.277), channel_id=1, source_target_pairs={{1,0},{2,1},{3,2},{4,3},{5,4},{6,5},{7,6},{9,8},{10,9},{11,10},{12... | collective-permute-start | bytes 4718600 | tf_op jit(solution)/shard_map/ppermute | solution.py:16
  30.3 129.4 %collective-permute-start = (bf16[4,256,768]{2,1,0:T(8,128)(2,1)}, bf16[4,256,768]{2,1,0:T(8,128)(2,1)}, u32[]{:S(2)}, u32[]{:S(2)}) collective-permute-start(bf16[4,256,768]{2,1,0:T(8,128)(2,1)} %get-tuple-element.277), channel_id=1, source_target_pairs={{0,1},{1,2},{2,3},{3,4},{4,5},{5,6},{6,7},{8,9},{9,10},{10,11},{11... | collective-permute-start | bytes 4718600 | tf_op jit(solution)/shard_map/ppermute | solution.py:16
  183.3 10.4 %copy-start.13 = (f32[2,2,12,256]{3,2,1,0:T(8,128)}, f32[2,2,12,256]{3,2,1,0:T(8,128)S(1)}, u32[]{:S(2)}) copy-start(f32[2,2,12,256]{3,2,1,0:T(8,128)S(1)} %get-tuple-element.476) | copy-start | bytes 147460 | tf_op jit(solution)/shard_map/while
  206.9 10.4 %copy-start.13 = (f32[2,2,12,256]{3,2,1,0:T(8,128)}, f32[2,2,12,256]{3,2,1,0:T(8,128)S(1)}, u32[]{:S(2)}) copy-start(f32[2,2,12,256]{3,2,1,0:T(8,128)S(1)} %get-tuple-element.476) | copy-start | bytes 147460 | tf_op jit(solution)/shard_map/while
  222.2 11.9 %copy-start.6 = (f32[4,256,768]{2,1,0:T(8,128)}, f32[4,256,768]{2,1,0:T(8,128)S(1)}, u32[]{:S(2)}) copy-start(f32[4,256,768]{2,1,0:T(8,128)S(1)} %get-tuple-element.285) | copy-start | bytes 9437188
  222.2 11.9 %copy-start.16 = (f32[4,256]{1,0:T(4,128)}, f32[4,256]{1,0:T(4,128)S(1)}, u32[]{:S(2)}) copy-start(f32[4,256]{1,0:T(4,128)S(1)} %broadcast_multiply_fusion.4) | copy-start | bytes 12292
  222.7 11.4 %copy-start.21 = (f32[4,256]{1,0:T(4,128)}, f32[4,256]{1,0:T(4,128)S(1)}, u32[]{:S(2)}) copy-start(f32[4,256]{1,0:T(4,128)S(1)} %add_rsqrt_fusion) | copy-start | bytes 12292
  234.1 28.7 %copy-start.8 = (f32[4,256,3072]{2,1,0:T(8,128)}, f32[4,256,3072]{2,1,0:T(8,128)S(1)}, u32[]{:S(2)}) copy-start(f32[4,256,3072]{2,1,0:T(8,128)S(1)} %get-tuple-element.286) | copy-start | bytes 37748740
  315.9 28.5 %slice-start = ((s8[4718592]{0:T(1024)(128)(4,1)}), s8[524288]{0:T(1024)(128)(4,1)S(1)}, s32[]{:S(2)}) async-start(s8[4718592]{0:T(1024)(128)(4,1)} %bitcast.172), calls=%async_computation.1 | async-start | bytes 1048576 | tf_op jit(solution)/shard_map/while
  330.9 13.5 %slice-start.1 = ((s8[4718592]{0:T(1024)(128)(4,1)}), s8[4194304]{0:T(1024)(128)(4,1)S(1)}, s32[]{:S(2)}) async-start(s8[4718592]{0:T(1024)(128)(4,1)} %bitcast.172), calls=%async_computation.2 | async-start | bytes 8388608 | tf_op jit(solution)/shard_map/while
  372.9 28.5 %slice-start = ((s8[4718592]{0:T(1024)(128)(4,1)}), s8[524288]{0:T(1024)(128)(4,1)S(1)}, s32[]{:S(2)}) async-start(s8[4718592]{0:T(1024)(128)(4,1)} %bitcast.172), calls=%async_computation.1 | async-start | bytes 1048576 | tf_op jit(solution)/shard_map/while
  388.0 13.5 %slice-start.1 = ((s8[4718592]{0:T(1024)(128)(4,1)}), s8[4194304]{0:T(1024)(128)(4,1)S(1)}, s32[]{:S(2)}) async-start(s8[4718592]{0:T(1024)(128)(4,1)} %bitcast.172), calls=%async_computation.2 | async-start | bytes 8388608 | tf_op jit(solution)/shard_map/while
  425.1 107.3 %collective-permute-start.6 = (bf16[4,256,768]{2,1,0:T(8,128)(2,1)}, bf16[4,256,768]{2,1,0:T(8,128)(2,1)}, u32[]{:S(2)}, u32[]{:S(2)}) collective-permute-start(bf16[4,256,768]{2,1,0:T(8,128)(2,1)} %get-tuple-element.273), channel_id=1, source_target_pairs={{1,0},{2,1},{3,2},{4,3},{5,4},{6,5},{7,6},{9,8},{10,9},{11,10},{12... | collective-permute-start | bytes 4718600 | tf_op jit(solution)/shard_map/ppermute | solution.py:16
  429.3 103.1 %collective-permute-start.7 = (bf16[4,256,768]{2,1,0:T(8,128)(2,1)}, bf16[4,256,768]{2,1,0:T(8,128)(2,1)}, u32[]{:S(2)}, u32[]{:S(2)}) collective-permute-start(bf16[4,256,768]{2,1,0:T(8,128)(2,1)} %get-tuple-element.274), channel_id=1, source_target_pairs={{0,1},{1,2},{2,3},{3,4},{4,5},{5,6},{6,7},{8,9},{9,10},{10,11},{11... | collective-permute-start | bytes 4718600 | tf_op jit(solution)/shard_map/ppermute | solution.py:16
  447.1 118.4 %collective-permute-start.4 = (bf16[4,256,768]{2,1,0:T(8,128)(2,1)}, bf16[4,256,768]{2,1,0:T(8,128)(2,1)}, u32[]{:S(2)}, u32[]{:S(2)}) collective-permute-start(bf16[4,256,768]{2,1,0:T(8,128)(2,1)} %get-tuple-element.271), channel_id=1, source_target_pairs={{1,0},{2,1},{3,2},{4,3},{5,4},{6,5},{7,6},{9,8},{10,9},{11,10},{12... | collective-permute-start | bytes 4718600 | tf_op jit(solution)/shard_map/ppermute | solution.py:16
  451.8 113.8 %collective-permute-start.5 = (bf16[4,256,768]{2,1,0:T(8,128)(2,1)}, bf16[4,256,768]{2,1,0:T(8,128)(2,1)}, u32[]{:S(2)}, u32[]{:S(2)}) collective-permute-start(bf16[4,256,768]{2,1,0:T(8,128)(2,1)} %get-tuple-element.272), channel_id=1, source_target_pairs={{0,1},{1,2},{2,3},{3,4},{4,5},{5,6},{6,7},{8,9},{9,10},{10,11},{11... | collective-permute-start | bytes 4718600 | tf_op jit(solution)/shard_map/ppermute | solution.py:16
  535.7 33.2 %copy-start.5 = (f32[4,256,768]{2,1,0:T(8,128)S(1)}, f32[4,256,768]{2,1,0:T(8,128)}, u32[]{:S(2)}) copy-start(f32[4,256,768]{2,1,0:T(8,128)} %copy-done.4) | copy-start | bytes 9437188
  535.8 33.2 %copy-start.11 = (bf16[4,256,768]{2,1,0:T(8,128)(2,1)S(1)}, bf16[4,256,768]{2,1,0:T(8,128)(2,1)}, u32[]{:S(2)}) copy-start(bf16[4,256,768]{2,1,0:T(8,128)(2,1)} %copy.44) | copy-start | bytes 4718596
  535.8 33.2 %copy-start.15 = (f32[4,256]{1,0:T(4,128)S(1)}, f32[4,256]{1,0:T(4,128)}, u32[]{:S(2)}) copy-start(f32[4,256]{1,0:T(4,128)} %copy-done.14) | copy-start | bytes 12292
  535.8 33.2 %copy-start.20 = (f32[4,256]{1,0:T(4,128)S(1)}, f32[4,256]{1,0:T(4,128)}, u32[]{:S(2)}) copy-start(f32[4,256]{1,0:T(4,128)} %copy-done.19) | copy-start | bytes 12292
  535.8 33.2 %copy-start.35 = (f32[768]{0:T(1024)S(1)}, f32[768]{0:T(1024)}, u32[]{:S(2)}) copy-start(f32[768]{0:T(1024)} %param.25) | copy-start | bytes 9220
  (35 other events, 160.0 us)
Sparse Core Ops, SparseCore 0:
  578.8 127.6 all-reduce.1
where the time goes:
time: 721 us; the launch traced here: 715 us
  waiting for transfers between devices  323 us (45%)
  matrix products  173 us (24%)
  other arithmetic  102 us (14%)
  local copies, waits for them, and re-layouts  76.2 us (11%)
  starting transfers between devices  25.3 us (4%)
  between operations  14.9 us (2%)
    ppermute x8, waiting for transfers between devices, passed_along(): return lax.ppermute(block, axis, route)  209 us
    psum x1, waiting for transfers between devices, body(): prompt_gradient = lax.psum(prompt_part, ('batch', 'seq'))  114 us
    dot_general x2, matrix products, backward_block(): jnp.einsum('gqhd,gkhd->ghqk', grad_blk, value_blk, preferred_element_type...  30 us
    another operation x1, other arithmetic, body(): jax.nn.gelu(inner, approximate=False)  28.7 us
    convert_element_type x2, other arithmetic, backward_block(): score_grad = (attention_weights * (prob_grad - inner)).astype(jnp.bfloat16)  27 us
    ppermute x8, starting transfers between devices, passed_along(): return lax.ppermute(block, axis, route)  25.2 us
    dot_general x2, matrix products, forward_block(): jnp.einsum('vbta,vabj->vtbj', attention_weights, value_blk, preferred_ele...  20.8 us
    dot_general x1, matrix products, body(): jnp.einsum('rsf,df->rsd', upper_grad, w_up, preferred_element_type=jnp.fl...  20.7 us
  transfers between devices with their start and end apart: 9, of which 6 were waited for; matrix products, arithmetic and copies ran while one was open for 8% of the time, Pallas kernels for 0%

commit v1 on v0

--- a/solution.py
+++ b/solution.py
@@ -223,7 +223,7 @@
     inserted_grad = hidden1_grad + norm_back(normed1_grad, normal1, inverse1, ln1_gain)
     token_gradient = jnp.where(is_prompt, 0.0, inserted_grad).astype(jnp.bfloat16)
     prompt_part = jnp.einsum("rsn,rsd->nd", one_hot, inserted_grad, precision=lax.Precision.HIGHEST)
-    prompt_gradient = lax.psum(prompt_part, ("batch", "seq"))
+    prompt_gradient = lax.all_gather(prompt_part, ("batch", "seq")).sum(axis=0)
     return (output, token_gradient, prompt_gradient)
 
 

time: 721 us -> 664 us (0.921)
  waiting for transfers between devices: 323 us -> 262 us
    psum x1 -> x0, waiting for transfers between devices: 114 us -> none  [body(): prompt_gradient = lax.psum(prompt_part, ('batch', 'seq'))]
    all_gather x0 -> x1, waiting for transfers between devices: none -> 53.4 us  [body(): prompt_gradient = lax.all_gather(prompt_part, ('batch', 'seq')).sum(axis=0)]
  transfers between devices with their start and end apart: 9 -> 9, of which waited for: 6 -> 6; matrix products, arithmetic and copies ran while one was open for 8% -> 9% of each run, Pallas kernels for 0% -> 0%
where the time goes in v1:
time: 664 us; the launch traced here: 657 us
  waiting for transfers between devices  262 us (39%)
  matrix products  173 us (26%)
  other arithmetic  105 us (16%)
  local copies, waits for them, and re-layouts  74.6 us (11%)
  starting transfers between devices  25.3 us (4%)
  between operations  14.9 us (2%)
    ppermute x8, waiting for transfers between devices, passed_along(): return lax.ppermute(block, axis, route)  209 us
    all_gather x1, waiting for transfers between devices, body(): prompt_gradient = lax.all_gather(prompt_part, ('batch', 'seq')).sum(axis=0)  53.4 us
    dot_general x2, matrix products, backward_block(): jnp.einsum('gqhd,gkhd->ghqk', grad_blk, value_blk, preferred_element_type...  30 us
    another operation x1, other arithmetic, body(): jax.nn.gelu(inner, approximate=False)  28.7 us
    convert_element_type x2, other arithmetic, backward_block(): score_grad = (attention_weights * (prob_grad - inner)).astype(jnp.bfloat16)  27 us
    ppermute x8, starting transfers between devices, passed_along(): return lax.ppermute(block, axis, route)  25.2 us
    dot_general x2, matrix products, forward_block(): jnp.einsum('vbta,vabj->vtbj', attention_weights, value_blk, preferred_ele...  20.8 us
    dot_general x1, matrix products, body(): jnp.einsum('rsf,df->rsd', upper_grad, w_up, preferred_element_type=jnp.fl...  20.7 us
  transfers between devices with their start and end apart: 9, of which 6 were waited for; matrix products, arithmetic and copies ran while one was open for 9% of the time, Pallas kernels for 0%

profile of v1, /device:TPU:8, one launch (start us, length us, event | category | flops | bytes accessed | tf_op | source)
XLA Modules:
  0.0 657.0 jit_solution(6317752355086786806)
XLA Ops:
  45.8 81.3 %collective-permute-done.3 = bf16[4,256,768]{2,1,0:T(8,128)(2,1)} collective-permute-done((bf16[4,256,768]{2,1,0:T(8,128)(2,1)}, bf16[4,256,768]{2,1,0:T(8,128)(2,1)}, u32[]{:S(2)}, u32[]{:S(2)}) %collective-permute-start.3) | collective-permute-done | bytes 1572896 | tf_op jit(solution)/shard_map/ppermute | solution.py:16
  131.0 6.6 %copy.49 = bf16[4,768,768]{1,2,0:T(8,128)(2,1)} copy(bf16[4,768,768]{2,1,0:T(8,128)(2,1)} %pad_maximum_fusion.1) | data formatting | bytes 9437184 | tf_op jit(solution)/shard_map/concatenate | solution.py:104
  137.6 22.0 %collective-permute-done.1 = bf16[4,256,768]{2,1,0:T(8,128)(2,1)} collective-permute-done((bf16[4,256,768]{2,1,0:T(8,128)(2,1)}, bf16[4,256,768]{2,1,0:T(8,128)(2,1)}, u32[]{:S(2)}, u32[]{:S(2)}) %collective-permute-start.1) | collective-permute-done | bytes 1572896 | tf_op jit(solution)/shard_map/ppermute | solution.py:16
  163.6 6.6 %copy.45 = bf16[4,768,768]{1,2,0:T(8,128)(2,1)} copy(bf16[4,768,768]{2,1,0:T(8,128)(2,1)} %pad_maximum_fusion) | data formatting | bytes 9437184 | tf_op jit(solution)/shard_map/concatenate | solution.py:105
  170.2 47.5 %while.28 = (s32[]{:T(128)}, bf16[2,2,256,12,64]{2,4,3,1,0:T(8,128)(2,1)}, f32[2,2,12,256]{3,2,1,0:T(8,128)}, bf16[2,2,768,12,64]{2,4,3,1,0:T(8,128)(2,1)}, s32[...) while((s32[]{:T(128)}, ...), condition=%wide.region_5.6_spmd.clone, body=%wide.region_2.5_spmd.clone.sunk | while | flops 1261628160 | bytes 141033712 | solution.py:137
  183.3 10.4 %fusion.152 = bf16[2,2,256,12,64]{2,4,3,1,0:T(8,128)(2,1)} fusion(bf16[2,2,256,12,64]{2,4,3,1,0:T(8,128)(2,1)} %get-tuple-element.464, s32[]{:T(128)S(6)} %copy.66, f32[2,12,256,768]{3,2,1,0:T(8,128)} %copy-done.2, f32[2,12,256]{2,1,0:T(8,128)S(1)} %get-tuple-element.433, pred[2,256,768]{2,1,0:T(8,128)(4,1)S(1)} %and_or_fusion.4, ...), kind=kOutput, calls=%fused_computation.17.clone.1 | convolution fusion | flops 623247360 | bytes 22438912 | tf_op jit(solution)/shard_map/while/body/eval_jaxpr/vbta,vabj->vtbj/dot_general | solution.py:132
  206.9 10.4 %fusion.152 = bf16[2,2,256,12,64]{2,4,3,1,0:T(8,128)(2,1)} fusion(bf16[2,2,256,12,64]{2,4,3,1,0:T(8,128)(2,1)} %get-tuple-element.464, s32[]{:T(128)S(6)} %copy.66, f32[2,12,256,768]{3,2,1,0:T(8,128)} %copy-done.2, f32[2,12,256]{2,1,0:T(8,128)S(1)} %get-tuple-element.433, pred[2,256,768]{2,1,0:T(8,128)(4,1)S(1)} %and_or_fusion.4, ...), kind=kOutput, calls=%fused_computation.17.clone.1 | convolution fusion | flops 623247360 | bytes 22438912 | tf_op jit(solution)/shard_map/while/body/eval_jaxpr/vbta,vabj->vtbj/dot_general | solution.py:132
  222.8 11.3 %fusion.95 = (u8[256,3072]{1,0:T(8,128)(4,1)S(1)}, u8[256,3072]{1,0:T(8,128)(4,1)S(1)}, f32[4,256,3072]{2,1,0:T(8,128)S(1)}) fusion(f32[3072]{0:T(1024)S(1)} %copy-done.29, bf16[768,3072]{1,0:T(8,128)(2,1)} %param.33, f32[4,256,768]{2,1,0:T(8,128)S(1)} %get-tuple-element.285, f32[768]{0:T(1024)S(1)} %copy-done.39, f32[768]{0:T(1024)S(1)} %copy-done.36, ...), kind=kOutput, calls=%fused_computation.138 | convolution fusion | flops 4878237696 | bytes 22046720 | tf_op jit(solution)/shard_map/rsd,df->rsf/dot_general | solution.py:148
  234.1 28.7 %fusion.63 = f32[4,256,3072]{2,1,0:T(8,128)} fusion(f32[4,256,3072]{2,1,0:T(8,128)S(1)} %get-tuple-element.286, f32[3072]{0:T(1024)S(1)} %copy-done.29, u8[256,3072]{1,0:T(8,128)(4,1)S(1)} %get-tuple-element.206, u8[256,3072]{1,0:T(8,128)(4,1)S(1)} %get-tuple-element.205), kind=kLoop, calls=%fused_computation.76 | loop fusion | flops 213909504 | bytes 26750976 | tf_op jit(solution)/shard_map/jvp()/erfc | solution.py:149
  262.8 20.7 %multiply_reduce_fusion.6 = (f32[4,256]{1,0:T(4,128)}, f32[4,256]{1,0:T(4,128)}, f32[4,256,768]{2,1,0:T(8,128)}) fusion(f32[768]{0:T(1024)} %param.31, f32[4,256]{1,0:T(4,128)} %copy-done.21, f32[4,256,768]{2,1,0:T(8,128)} %copy-done.6, f32[4,256]{1,0:T(4,128)} %copy-done.16, bf16[768,3072]{1,0:T(8,128)(2,1)} %param.33, f32[4,256,3072]{2,1,0:T(8,128)} %fusion.63, ...), kind=kOutput, calls=%fused_computation.142 | convolution fusion | flops 9717938176 | bytes 42503168 | tf_op jit(solution)/shard_map/rsf,df->rsd/dot_general | solution.py:161
  285.4 7.0 %convolution_convert_fusion = bf16[4,256,768]{2,1,0:T(8,128)(2,1)} fusion(bf16[768,768]{1,0:T(8,128)(2,1)} %param.29, bf16[4,256,768]{2,1,0:T(8,128)(2,1)} %param.37, f32[4,256,768]{2,1,0:T(8,128)} %get-tuple-element.287, f32[4,256,768]{2,1,0:T(8,128)} %copy-done.6, f32[4,256]{1,0:T(4,128)S(1)} %broadcast_multiply_fusion.2, ...), kind=kOutput, calls=%fused_computation.143 | convolution fusion | flops 1217396736 | bytes 10640384 | tf_op jit(solution)/shard_map/rse,de->rsd/dot_general | solution.py:163
  295.0 114.5 %while.29 = (s32[]{:T(128)}, bf16[2,2,256,12,64]{2,4,3,1,0:T(8,128)(2,1)}, f32[2,2,768,12,64]{2,4,3,1,0:T(8,128)}, f32[2,2,768,12,64]{2,4,3,1,0:T(8,128)}, bf16[...) while((s32[]{:T(128)}, ...), condition=%wide.region_12.13_spmd.clone, body=%wide.region_10.12_spmd.clone.sunk | while | flops 3093621504 | bytes 260910336 | solution.py:191
  308.2 7.7 %bitcast_dynamic-update-slice_fusion.11 = f32[2,2,768,12,64]{2,4,3,1,0:T(8,128)} fusion(f32[2,2,768,12,64]{2,4,3,1,0:T(8,128)} %get-tuple-element.502, s32[]{:T(128)S(6)} %copy.76, f32[2,12,256,768]{3,2,1,0:T(8,128)S(1)} %fusion.161, f32[2,12,256]{2,1,0:T(8,128)S(1)} %dynamic-slice_bitcast_fusion.9, pred[2,256,768]{2,1,0:T(8,128)(4,1)S(1)} %and_or_fusion.5, ...), kind=kOutput, calls=%fused_computation.40.clone.1 | convolution fusion | flops 622854144 | bytes 24798208 | tf_op jit(solution)/shard_map/while/body/eval_jaxpr/ghqk,gqhd->gkhd/dot_general | solution.py:172
  315.8 15.0 %multiply_reduce_fusion.8 = (f32[2,12,256]{2,1,0:T(8,128)S(1)}, f32[2,12,256,768]{3,2,1,0:T(8,128)}) fusion(f32[2,12,256,768]{3,2,1,0:T(8,128)} %copy-done.1, f32[2,12,256]{2,1,0:T(8,128)S(1)} %dynamic-slice_bitcast_fusion.9, pred[2,256,768]{2,1,0:T(8,128)(4,1)S(1)} %and_or_fusion.5, bf16[2,2,768,12,64]{2,4,3,1,0:T(8,128)(2,1)} %get-tuple-element.524, ...), kind=kOutput, calls=%fused_computation.32.clone.1 | convolution fusion | flops 627566592 | bytes 41337856 | tf_op jit(solution)/shard_map/while/body/eval_jaxpr/gqhd,gkhd->ghqk/dot_general | solution.py:178
  330.9 13.5 %multiply_convert_fusion.6 = bf16[2,12,256,768]{3,2,1,0:T(8,128)(2,1)S(1)} fusion(f32[2,12,256,768]{3,2,1,0:T(8,128)} %get-tuple-element.450, f32[2,12,256,768]{3,2,1,0:T(8,128)} %copy-done.1, f32[2,12,256]{2,1,0:T(8,128)S(1)} %get-tuple-element.451, f32[2,12,256]{2,1,0:T(8,128)S(1)} %dynamic-slice_bitcast_fusion.9, ...), kind=kLoop, calls=%fused_computation.31.clone.1 | loop fusion | flops 28311552 | bytes 47628288 | tf_op jit(solution)/shard_map/while/body/eval_jaxpr/convert_element_type | solution.py:182
  365.2 7.7 %bitcast_dynamic-update-slice_fusion.11 = f32[2,2,768,12,64]{2,4,3,1,0:T(8,128)} fusion(f32[2,2,768,12,64]{2,4,3,1,0:T(8,128)} %get-tuple-element.502, s32[]{:T(128)S(6)} %copy.76, f32[2,12,256,768]{3,2,1,0:T(8,128)S(1)} %fusion.161, f32[2,12,256]{2,1,0:T(8,128)S(1)} %dynamic-slice_bitcast_fusion.9, pred[2,256,768]{2,1,0:T(8,128)(4,1)S(1)} %and_or_fusion.5, ...), kind=kOutput, calls=%fused_computation.40.clone.1 | convolution fusion | flops 622854144 | bytes 24798208 | tf_op jit(solution)/shard_map/while/body/eval_jaxpr/ghqk,gqhd->gkhd/dot_general | solution.py:172
  372.9 15.0 %multiply_reduce_fusion.8 = (f32[2,12,256]{2,1,0:T(8,128)S(1)}, f32[2,12,256,768]{3,2,1,0:T(8,128)}) fusion(f32[2,12,256,768]{3,2,1,0:T(8,128)} %copy-done.1, f32[2,12,256]{2,1,0:T(8,128)S(1)} %dynamic-slice_bitcast_fusion.9, pred[2,256,768]{2,1,0:T(8,128)(4,1)S(1)} %and_or_fusion.5, bf16[2,2,768,12,64]{2,4,3,1,0:T(8,128)(2,1)} %get-tuple-element.524, ...), kind=kOutput, calls=%fused_computation.32.clone.1 | convolution fusion | flops 627566592 | bytes 41337856 | tf_op jit(solution)/shard_map/while/body/eval_jaxpr/gqhd,gkhd->ghqk/dot_general | solution.py:178
  387.9 13.5 %multiply_convert_fusion.6 = bf16[2,12,256,768]{3,2,1,0:T(8,128)(2,1)S(1)} fusion(f32[2,12,256,768]{3,2,1,0:T(8,128)} %get-tuple-element.450, f32[2,12,256,768]{3,2,1,0:T(8,128)} %copy-done.1, f32[2,12,256]{2,1,0:T(8,128)S(1)} %get-tuple-element.451, f32[2,12,256]{2,1,0:T(8,128)S(1)} %dynamic-slice_bitcast_fusion.9, ...), kind=kLoop, calls=%fused_computation.31.clone.1 | loop fusion | flops 28311552 | bytes 47628288 | tf_op jit(solution)/shard_map/while/body/eval_jaxpr/convert_element_type | solution.py:182
  409.5 9.6 %copy.54 = f32[4,768,768]{2,1,0:T(8,128)} copy(f32[4,768,768]{1,2,0:T(8,128)} %bitcast.178) | data formatting | bytes 18874368 | tf_op jit(solution)/shard_map/reshape | solution.py:205
  431.4 9.7 %copy.52 = f32[4,768,768]{2,1,0:T(8,128)} copy(f32[4,768,768]{1,2,0:T(8,128)} %bitcast.179) | data formatting | bytes 18874368 | tf_op jit(solution)/shard_map/reshape | solution.py:204
  456.4 76.0 %collective-permute-done.6 = bf16[4,256,768]{2,1,0:T(8,128)(2,1)} collective-permute-done((bf16[4,256,768]{2,1,0:T(8,128)(2,1)}, bf16[4,256,768]{2,1,0:T(8,128)(2,1)}, u32[]{:S(2)}, u32[]{:S(2)}) %collective-permute-start.6) | collective-permute-done | bytes 1572896 | tf_op jit(solution)/shard_map/ppermute | solution.py:16
  535.8 29.7 %collective-permute-done.4 = bf16[4,256,768]{2,1,0:T(8,128)(2,1)} collective-permute-done((bf16[4,256,768]{2,1,0:T(8,128)(2,1)}, bf16[4,256,768]{2,1,0:T(8,128)(2,1)}, u32[]{:S(2)}, u32[]{:S(2)}) %collective-permute-start.4) | collective-permute-done | bytes 1572896 | tf_op jit(solution)/shard_map/ppermute | solution.py:16
  578.7 14.3 %add_convert_fusion.3 = bf16[4,256,768]{2,1,0:T(8,128)(2,1)} fusion(f32[4,256,768]{2,1,0:T(8,128)} %copy-done.6, bf16[3072,768]{1,0:T(8,128)(2,1)} %param.35, f32[4,256,3072]{2,1,0:T(8,128)} %fusion.63, f32[4,256,3072]{2,1,0:T(8,128)} %copy-done.8, f32[3072]{0:T(1024)S(1)} %copy-done.30, f32[768]{0:T(1024)S(1)} %copy-done.40), kind=kOutput, calls=%fused_computation.130 | convolution fusion | flops 4846780416 | bytes 34618368 | tf_op jit(solution)/shard_map/rsf,fd->rsd/dot_general | solution.py:153
  593.1 53.4 %all-gather.4.cloned.1.call-done = f32[32,50,768]{2,1,0:T(8,128)} async-done(((f32[1,50,768]{2,1,0:T(8,128)}), f32[32,50,768]{2,1,0:T(8,128)}) %all-gather.4.cloned.1.call-update) | async-done | bytes 4915216 | tf_op jit(solution)/shard_map/all_gather | solution.py:226
  (200 shorter events, 171.0 us)
Async XLA Ops:
  7.2 639.3 %all-gather.4.cloned.1.call-start = ((), (), s32[]{:S(2)}) async-start(), calls=%async_computation | async-start | bytes 5677056 | tf_op jit(solution)/shard_map/all_gather | solution.py:226
  20.2 106.9 %collective-permute-start.3 = (bf16[4,256,768]{2,1,0:T(8,128)(2,1)}, bf16[4,256,768]{2,1,0:T(8,128)(2,1)}, u32[]{:S(2)}, u32[]{:S(2)}) collective-permute-start(bf16[4,256,768]{2,1,0:T(8,128)(2,1)} %get-tuple-element.275), channel_id=1, source_target_pairs={{1,0},{2,1},{3,2},{4,3},{5,4},{6,5},{7,6},{9,8},{10,9},{11,10},{12... | collective-permute-start | bytes 4718600 | tf_op jit(solution)/shard_map/ppermute | solution.py:16
  23.5 103.6 %collective-permute-start.2 = (bf16[4,256,768]{2,1,0:T(8,128)(2,1)}, bf16[4,256,768]{2,1,0:T(8,128)(2,1)}, u32[]{:S(2)}, u32[]{:S(2)}) collective-permute-start(bf16[4,256,768]{2,1,0:T(8,128)(2,1)} %get-tuple-element.275), channel_id=1, source_target_pairs={{0,1},{1,2},{2,3},{3,4},{4,5},{5,6},{6,7},{8,9},{9,10},{10,11},{11... | collective-permute-start | bytes 4718600 | tf_op jit(solution)/shard_map/ppermute | solution.py:16
  26.0 133.6 %collective-permute-start.1 = (bf16[4,256,768]{2,1,0:T(8,128)(2,1)}, bf16[4,256,768]{2,1,0:T(8,128)(2,1)}, u32[]{:S(2)}, u32[]{:S(2)}) collective-permute-start(bf16[4,256,768]{2,1,0:T(8,128)(2,1)} %get-tuple-element.277), channel_id=1, source_target_pairs={{1,0},{2,1},{3,2},{4,3},{5,4},{6,5},{7,6},{9,8},{10,9},{11,10},{12... | collective-permute-start | bytes 4718600 | tf_op jit(solution)/shard_map/ppermute | solution.py:16
  30.3 129.4 %collective-permute-start = (bf16[4,256,768]{2,1,0:T(8,128)(2,1)}, bf16[4,256,768]{2,1,0:T(8,128)(2,1)}, u32[]{:S(2)}, u32[]{:S(2)}) collective-permute-start(bf16[4,256,768]{2,1,0:T(8,128)(2,1)} %get-tuple-element.277), channel_id=1, source_target_pairs={{0,1},{1,2},{2,3},{3,4},{4,5},{5,6},{6,7},{8,9},{9,10},{10,11},{11... | collective-permute-start | bytes 4718600 | tf_op jit(solution)/shard_map/ppermute | solution.py:16
  183.3 10.4 %copy-start.13 = (f32[2,2,12,256]{3,2,1,0:T(8,128)}, f32[2,2,12,256]{3,2,1,0:T(8,128)S(1)}, u32[]{:S(2)}) copy-start(f32[2,2,12,256]{3,2,1,0:T(8,128)S(1)} %get-tuple-element.476) | copy-start | bytes 147460 | tf_op jit(solution)/shard_map/while
  206.9 10.4 %copy-start.13 = (f32[2,2,12,256]{3,2,1,0:T(8,128)}, f32[2,2,12,256]{3,2,1,0:T(8,128)S(1)}, u32[]{:S(2)}) copy-start(f32[2,2,12,256]{3,2,1,0:T(8,128)S(1)} %get-tuple-element.476) | copy-start | bytes 147460 | tf_op jit(solution)/shard_map/while
  222.2 11.9 %copy-start.6 = (f32[4,256,768]{2,1,0:T(8,128)}, f32[4,256,768]{2,1,0:T(8,128)S(1)}, u32[]{:S(2)}) copy-start(f32[4,256,768]{2,1,0:T(8,128)S(1)} %get-tuple-element.285) | copy-start | bytes 9437188
  222.2 11.9 %copy-start.16 = (f32[4,256]{1,0:T(4,128)}, f32[4,256]{1,0:T(4,128)S(1)}, u32[]{:S(2)}) copy-start(f32[4,256]{1,0:T(4,128)S(1)} %broadcast_multiply_fusion.4) | copy-start | bytes 12292
  222.7 11.3 %copy-start.21 = (f32[4,256]{1,0:T(4,128)}, f32[4,256]{1,0:T(4,128)S(1)}, u32[]{:S(2)}) copy-start(f32[4,256]{1,0:T(4,128)S(1)} %add_rsqrt_fusion) | copy-start | bytes 12292
  234.1 28.7 %copy-start.8 = (f32[4,256,3072]{2,1,0:T(8,128)}, f32[4,256,3072]{2,1,0:T(8,128)S(1)}, u32[]{:S(2)}) copy-start(f32[4,256,3072]{2,1,0:T(8,128)S(1)} %get-tuple-element.286) | copy-start | bytes 37748740
  315.8 28.5 %slice-start = ((s8[4718592]{0:T(1024)(128)(4,1)}), s8[524288]{0:T(1024)(128)(4,1)S(1)}, s32[]{:S(2)}) async-start(s8[4718592]{0:T(1024)(128)(4,1)} %bitcast.173), calls=%async_computation.1 | async-start | bytes 1048576 | tf_op jit(solution)/shard_map/while
  330.9 13.5 %slice-start.1 = ((s8[4718592]{0:T(1024)(128)(4,1)}), s8[4194304]{0:T(1024)(128)(4,1)S(1)}, s32[]{:S(2)}) async-start(s8[4718592]{0:T(1024)(128)(4,1)} %bitcast.173), calls=%async_computation.2 | async-start | bytes 8388608 | tf_op jit(solution)/shard_map/while
  372.9 28.5 %slice-start = ((s8[4718592]{0:T(1024)(128)(4,1)}), s8[524288]{0:T(1024)(128)(4,1)S(1)}, s32[]{:S(2)}) async-start(s8[4718592]{0:T(1024)(128)(4,1)} %bitcast.173), calls=%async_computation.1 | async-start | bytes 1048576 | tf_op jit(solution)/shard_map/while
  387.9 13.5 %slice-start.1 = ((s8[4718592]{0:T(1024)(128)(4,1)}), s8[4194304]{0:T(1024)(128)(4,1)S(1)}, s32[]{:S(2)}) async-start(s8[4718592]{0:T(1024)(128)(4,1)} %bitcast.173), calls=%async_computation.2 | async-start | bytes 8388608 | tf_op jit(solution)/shard_map/while
  425.1 107.3 %collective-permute-start.6 = (bf16[4,256,768]{2,1,0:T(8,128)(2,1)}, bf16[4,256,768]{2,1,0:T(8,128)(2,1)}, u32[]{:S(2)}, u32[]{:S(2)}) collective-permute-start(bf16[4,256,768]{2,1,0:T(8,128)(2,1)} %get-tuple-element.273), channel_id=1, source_target_pairs={{1,0},{2,1},{3,2},{4,3},{5,4},{6,5},{7,6},{9,8},{10,9},{11,10},{12... | collective-permute-start | bytes 4718600 | tf_op jit(solution)/shard_map/ppermute | solution.py:16
  429.3 103.1 %collective-permute-start.7 = (bf16[4,256,768]{2,1,0:T(8,128)(2,1)}, bf16[4,256,768]{2,1,0:T(8,128)(2,1)}, u32[]{:S(2)}, u32[]{:S(2)}) collective-permute-start(bf16[4,256,768]{2,1,0:T(8,128)(2,1)} %get-tuple-element.274), channel_id=1, source_target_pairs={{0,1},{1,2},{2,3},{3,4},{4,5},{5,6},{6,7},{8,9},{9,10},{10,11},{11... | collective-permute-start | bytes 4718600 | tf_op jit(solution)/shard_map/ppermute | solution.py:16
  447.1 118.4 %collective-permute-start.4 = (bf16[4,256,768]{2,1,0:T(8,128)(2,1)}, bf16[4,256,768]{2,1,0:T(8,128)(2,1)}, u32[]{:S(2)}, u32[]{:S(2)}) collective-permute-start(bf16[4,256,768]{2,1,0:T(8,128)(2,1)} %get-tuple-element.271), channel_id=1, source_target_pairs={{1,0},{2,1},{3,2},{4,3},{5,4},{6,5},{7,6},{9,8},{10,9},{11,10},{12... | collective-permute-start | bytes 4718600 | tf_op jit(solution)/shard_map/ppermute | solution.py:16
  451.8 113.8 %collective-permute-start.5 = (bf16[4,256,768]{2,1,0:T(8,128)(2,1)}, bf16[4,256,768]{2,1,0:T(8,128)(2,1)}, u32[]{:S(2)}, u32[]{:S(2)}) collective-permute-start(bf16[4,256,768]{2,1,0:T(8,128)(2,1)} %get-tuple-element.272), channel_id=1, source_target_pairs={{0,1},{1,2},{2,3},{3,4},{4,5},{5,6},{6,7},{8,9},{9,10},{10,11},{11... | collective-permute-start | bytes 4718600 | tf_op jit(solution)/shard_map/ppermute | solution.py:16
  535.7 33.2 %copy-start.5 = (f32[4,256,768]{2,1,0:T(8,128)S(1)}, f32[4,256,768]{2,1,0:T(8,128)}, u32[]{:S(2)}) copy-start(f32[4,256,768]{2,1,0:T(8,128)} %copy-done.4) | copy-start | bytes 9437188
  535.7 33.2 %copy-start.11 = (bf16[4,256,768]{2,1,0:T(8,128)(2,1)S(1)}, bf16[4,256,768]{2,1,0:T(8,128)(2,1)}, u32[]{:S(2)}) copy-start(bf16[4,256,768]{2,1,0:T(8,128)(2,1)} %copy.56) | copy-start | bytes 4718596
  535.7 33.2 %copy-start.15 = (f32[4,256]{1,0:T(4,128)S(1)}, f32[4,256]{1,0:T(4,128)}, u32[]{:S(2)}) copy-start(f32[4,256]{1,0:T(4,128)} %copy-done.14) | copy-start | bytes 12292
  535.8 33.2 %copy-start.20 = (f32[4,256]{1,0:T(4,128)S(1)}, f32[4,256]{1,0:T(4,128)}, u32[]{:S(2)}) copy-start(f32[4,256]{1,0:T(4,128)} %copy-done.19) | copy-start | bytes 12292
  535.8 33.2 %copy-start.35 = (f32[768]{0:T(1024)S(1)}, f32[768]{0:T(1024)}, u32[]{:S(2)}) copy-start(f32[768]{0:T(1024)} %param.25) | copy-start | bytes 9220
  (35 other events, 160.0 us)
Sparse Core Ops, SparseCore 0:
  578.8 67.5 all-gather.3
